TPU v7x, 256 devices: a whole 4x4x8 slice. The times are simulated.
256 devices in a mesh: rows: 64 (over z, x, core), cols: 4 (over y).
Axes of the slice: x: 4, y: 4, z: 8, core: 2. Of those that a mesh axis runs over, the one named last changes fastest.
Arguments:
- source: float32 [8192, 32768], P('rows', 'cols'), may hold values from -6 to 6
- low_row: int32 [8192], replicated, may hold values from 0 to 8190, as said below
- weight_low: float32 [8192], replicated, may hold values from 0 to 1
Outputs:
- mercator: float32 [8192, 32768], P('rows', 'cols')
- level1: float32 [4096, 16384], P('rows', 'cols')
- level2: float32 [2048, 8192], P('rows', 'cols')
- level3: float32 [1024, 4096], P(('rows', 'cols'))
- level4: float32 [512, 2048], P(('rows', 'cols'))
Inputs may be any that keep to these rules, and one draw needn't show every extreme that they name: With t = 68 degrees in radians, E = ln tan(pi/4 + t/2), y = E * (1 - (2m + 1) / 16384) and lat = 2 atan(exp(y)) - pi/2, the base row of Mercator row m is floor((t - lat) / t * 8192 - 0.5) clipped to the range; low_row[m] differs from it by at most 2 and is then clipped to the range.
All inputs are finite; a program needn't handle non-finite values.
Results may differ from a plain program's by a relative error of at most 0.00007.
Values sent between devices are 32-bit elements; how exact they have to be, the bound alone decides.
A program may use at most 128 MiB of HBM per device.

v0:
```python
import math

import jax
import jax.numpy as jnp
from jax import lax
from jax.sharding import PartitionSpec as P


def blend(columns, low_row, weight_low):
    count = low_row.shape[0]
    both_rows = jnp.concatenate([low_row, low_row + 1], axis=0)
    fetched = jnp.take(columns, both_rows, axis=0)
    paired = fetched.reshape((2, count) + columns.shape[1:])
    scales = weight_low.reshape((-1,) + (1,) * (columns.ndim - 1))
    return scales * paired[0] + (1.0 - scales) * paired[1]


def halve(picture):
    height = picture.shape[0]
    width = picture.shape[1]
    stacked = picture.reshape(height // 2, 2, width)
    row_sums = stacked[:, 0, :] + stacked[:, 1, :]
    block = math.gcd(width, 256)
    inputs = lax.broadcasted_iota(jnp.int32, (block, block // 2), 0)
    outputs = lax.broadcasted_iota(jnp.int32, (block, block // 2), 1)
    pairing = jnp.where(inputs // 2 == outputs, 0.25, 0.0).astype(jnp.float32)
    blocks = row_sums.reshape(height // 2, width // block, block)
    pooled = jnp.einsum(
        "rkb,bo->rko",
        blocks,
        pairing,
        precision=lax.Precision.HIGHEST,
        preferred_element_type=jnp.float32,
    )
    return pooled.reshape(height // 2, width // 2)


def body(source, low_row, weight_low):
    columns = lax.all_to_all(source, "rows", split_axis=1, concat_axis=0, tiled=True)
    blended = blend(columns, low_row, weight_low)
    mercator = lax.all_to_all(blended, "rows", split_axis=0, concat_axis=1, tiled=True)
    level1 = halve(mercator)
    level2 = halve(level1)
    level3 = halve(level2)
    level3_rows = lax.all_to_all(level3, "cols", split_axis=0, concat_axis=1, tiled=True)
    level4_rows = halve(level3_rows)
    return (mercator, level1, level2, level3_rows, level4_rows)


def solution(mesh):
    placed = (P("rows", "cols"), P(), P())
    return jax.shard_map(
        body,
        mesh=mesh,
        in_specs=placed,
        out_specs=(
            P("rows", "cols"),
            P("rows", "cols"),
            P("rows", "cols"),
            P(("rows", "cols"), None),
            P(("rows", "cols"), None),
        ),
        check_vma=False,
    )
```

profile of v0, /device:TPU:102, one launch (start us, length us, event | category | flops | bytes accessed | tf_op | source)
XLA Modules:
  0.0 332.7 jit_solution(13222126053294794500)
XLA Ops:
  0.6 4.8 %copy_bitcast_fusion = f32[128,64,128]{2,0,1:T(8,128)} fusion(f32[128,8192]{1,0:T(8,128)} %param.3), kind=kLoop, calls=%fused_computation.1 | loop fusion | bytes 8388608 | tf_op jit(solution)/shard_map/all_to_all | solution.py:39
  5.4 0.0 copy-start
  5.4 0.0 copy-start.1
  5.4 11.0 %all-to-all-start = ((f32[128,64,128]{2,0,1:T(8,128)}), f32[128,64,128]{2,0,1:T(8,128)}, u32[]{:S(2)}, u32[]{:S(2)}) async-start(f32[128,64,128]{2,0,1:T(8,128)} %copy_bitcast_fusion), calls=%async_computation | async-start | bytes 8388608 | tf_op jit(solution)/shard_map/all_to_all | solution.py:39
  16.4 0.0 copy-done
  16.5 0.0 copy-done.1
  16.5 0.1 compare_select_fusion
  16.6 92.7 %all-to-all-done = f32[128,64,128]{2,0,1:T(8,128)} async-done(((f32[128,64,128]{2,0,1:T(8,128)}), f32[128,64,128]{2,0,1:T(8,128)}, u32[]{:S(2)}, u32[]{:S(2)}) %all-to-all-start) | async-done | bytes 4194336 | tf_op jit(solution)/shard_map/all_to_all | solution.py:39
  109.3 56.6 %gather_fusion = f32[16384,128]{1,0:T(8,128)} fusion(f32[8192,128]{1,0:T(8,128)} %bitcast.2, s32[16384]{0:T(1024)S(1)} %broadcast_clamp_fusion), kind=kCustom, calls=%fused_computation | custom fusion | bytes 16842752 | tf_op jit(solution)/shard_map/jit(_take)/gather | solution.py:12
  165.9 11.8 %broadcast_select_fusion = f32[16384,128]{1,0:T(8,128)S(1)} fusion(f32[16384,128]{1,0:T(8,128)} %gather_fusion, pred[16384]{0:T(1024)(128)(4,1)S(1)} %compare_and_fusion), kind=kLoop, calls=%fused_computation.3 | loop fusion | flops 2097152 | bytes 16793600 | tf_op jit(solution)/shard_map/jit(_take)/select_n | solution.py:12
  177.7 0.5 fusion.45
  178.2 3.8 %multiply_add_fusion = f32[64,128,128]{2,1,0:T(8,128)} fusion(f32[64,128,128]{2,1,0:T(8,128)S(1)} %bitcast.59, f32[64,128,128]{2,1,0:T(8,128)S(1)} %bitcast.58, f32[64,128]{1,0:T(8,128)S(1)} %subtract_bitcast_fusion, f32[64,128]{1,0:T(8,128)S(1)} %bitcast.75), kind=kLoop, calls=%fused_computation.2 | loop fusion | flops 3145728 | bytes 12648448 | tf_op jit(solution)/shard_map/add | solution.py:15
  182.0 9.1 %all-to-all-start.1 = ((f32[64,128,128]{2,1,0:T(8,128)}), f32[64,128,128]{2,1,0:T(8,128)}, u32[]{:S(2)}, u32[]{:S(2)}) async-start(f32[64,128,128]{2,1,0:T(8,128)} %multiply_add_fusion), calls=%async_computation.1 | async-start | bytes 8388608 | tf_op jit(solution)/shard_map/all_to_all | solution.py:41
  191.1 92.7 %all-to-all-done.1 = f32[64,128,128]{2,1,0:T(8,128)} async-done(((f32[64,128,128]{2,1,0:T(8,128)}), f32[64,128,128]{2,1,0:T(8,128)}, u32[]{:S(2)}, u32[]{:S(2)}) %all-to-all-start.1) | async-done | bytes 4194336 | tf_op jit(solution)/shard_map/all_to_all | solution.py:41
  283.8 6.6 %copy.26 = f32[128,64,128]{2,1,0:T(8,128)} copy(f32[128,64,128]{2,0,1:T(8,128)} %bitcast.11) | data formatting | bytes 8388608 | tf_op jit(solution)/shard_map/all_to_all | solution.py:41
  290.5 5.8 %reshape.168 = f32[64,2,8192]{2,1,0:T(2,128)} reshape(f32[128,64,128]{2,1,0:T(8,128)} %copy.26) | data formatting | bytes 8388608 | tf_op jit(solution)/shard_map/reshape | solution.py:21
  296.2 9.3 %fusion = f32[64,8192]{1,0:T(8,128)S(1)} fusion(f32[64,2,8192]{2,1,0:T(2,128)} %reshape.168), kind=kLoop, calls=%fused_computation.5 | loop fusion | flops 524288 | bytes 6291456 | tf_op jit(solution)/shard_map/add | solution.py:22
  305.5 0.6 copy.31
  306.1 1.9 fusion.8
  308.1 0.6 reshape_reshape.6
  308.6 1.6 fusion.1
  310.3 0.2 copy.33
  310.4 0.7 fusion.6
  311.1 0.1 reshape_reshape.7
  311.3 0.4 fusion.2
  311.7 0.4 fusion.4
  312.2 0.7 all_to_all.47
  312.8 4.5 %all-to-all-start.2 = ((f32[4,4,1024]{2,1,0:T(4,128)}), f32[4,4,1024]{2,1,0:T(4,128)S(1)}, u32[]{:S(2)}, u32[]{:S(2)}) async-start(f32[4,4,1024]{2,1,0:T(4,128)} %all_to_all.47), calls=%async_computation.2 | async-start | bytes 131072 | tf_op jit(solution)/shard_map/all_to_all | solution.py:45
  317.3 0.8 copy.47
  318.1 1.6 copy.46
  319.6 5.6 %copy.25 = f32[64,128,128]{1,2,0:T(8,128)} copy(f32[64,128,128]{2,1,0:T(8,128)} %all-to-all-done.1) | data formatting | bytes 8388608 | tf_op jit(solution)/shard_map/all_to_all | solution.py:41
  325.2 5.6 %copy.28 = f32[128,8192]{1,0:T(8,128)} copy(f32[128,8192]{0,1:T(8,128)} %bitcast.60) | data formatting | bytes 8388608
  330.8 0.0 all-to-all-done.2
  330.9 0.1 reshape.171
  331.0 0.1 fusion.36
  331.1 0.3 convolution_bitcast_fusion
  331.4 0.6 copy.48
  332.0 0.6 copy.50
  (8 shorter events, 0.1 us)
Async XLA Ops:
  5.4 11.0 %copy-start = (s32[8192]{0:T(1024)S(1)}, s32[8192]{0:T(1024)}, u32[]{:S(2)}) copy-start(s32[8192]{0:T(1024)} %param.4) | copy-start | bytes 98308
  5.4 11.1 %copy-start.1 = (f32[8192]{0:T(1024)S(1)}, f32[8192]{0:T(1024)}, u32[]{:S(2)}) copy-start(f32[8192]{0:T(1024)} %param.5) | copy-start | bytes 98308
  5.4 103.9 %all-to-all-start = ((f32[128,64,128]{2,0,1:T(8,128)}), f32[128,64,128]{2,0,1:T(8,128)}, u32[]{:S(2)}, u32[]{:S(2)}) async-start(f32[128,64,128]{2,0,1:T(8,128)} %copy_bitcast_fusion), calls=%async_computation | async-start | bytes 8388608 | tf_op jit(solution)/shard_map/all_to_all | solution.py:39
  182.0 101.8 %all-to-all-start.1 = ((f32[64,128,128]{2,1,0:T(8,128)}), f32[64,128,128]{2,1,0:T(8,128)}, u32[]{:S(2)}, u32[]{:S(2)}) async-start(f32[64,128,128]{2,1,0:T(8,128)} %multiply_add_fusion), calls=%async_computation.1 | async-start | bytes 8388608 | tf_op jit(solution)/shard_map/all_to_all | solution.py:41
  312.8 18.0 %all-to-all-start.2 = ((f32[4,4,1024]{2,1,0:T(4,128)}), f32[4,4,1024]{2,1,0:T(4,128)S(1)}, u32[]{:S(2)}, u32[]{:S(2)}) async-start(f32[4,4,1024]{2,1,0:T(4,128)} %all_to_all.47), calls=%async_computation.2 | async-start | bytes 131072 | tf_op jit(solution)/shard_map/all_to_all | solution.py:45
where the time goes:
time: 339 us; the launch traced here: 333 us
  waiting for transfers between devices  185 us (55%)
  local copies, waits for them, and re-layouts  91.4 us (27%)
  other arithmetic  27.1 us (8%)
  starting transfers between devices  24.5 us (7%)
  matrix products  3.4 us (1%)
    all_to_all x1, waiting for transfers between devices, body(): lax.all_to_all(blended, 'rows', split_axis=0, concat_axis=1, tiled=True)  92.7 us
    all_to_all x1, waiting for transfers between devices, body(): lax.all_to_all(source, 'rows', split_axis=1, concat_axis=0, tiled=True)  92.7 us
    gather x1, local copies, waits for them, and re-layouts, blend(): fetched = jnp.take(columns, both_rows, axis=0)  56.6 us
    all_to_all x2, local copies, waits for them, and re-layouts, body(): lax.all_to_all(blended, 'rows', split_axis=0, concat_axis=1, tiled=True)  12.2 us
    select_n x2, other arithmetic, blend(): fetched = jnp.take(columns, both_rows, axis=0)  11.8 us
    add x4, other arithmetic, halve(): row_sums = stacked[:, 0, :] + stacked[:, 1, :]  11.4 us
    all_to_all x1, starting transfers between devices, body(): lax.all_to_all(source, 'rows', split_axis=1, concat_axis=0, tiled=True)  11 us
    unnamed x12, local copies, waits for them, and re-layouts  10 us
  transfers between devices with their start and end apart: 3, of which 2 were waited for; matrix products, arithmetic and copies ran while one was open for 4% of the time, Pallas kernels for 0%

commit v1 on v0

v1 whole, which is shorter than its diff:
```python
import functools
import math

import jax
import jax.numpy as jnp
import numpy as np
from jax import lax
from jax.experimental import pallas as pl
from jax.experimental.pallas import tpu as pltpu
from jax.sharding import PartitionSpec as P

TOTAL = 8192
WIDTH = 8192
LINES = 128
DEVICES = 64
FIRST_BLENDED = 36
FIRST_KEPT = 61
CHUNKS = 4
CHUNK = WIDTH // CHUNKS
STEP = 1024

ROUTES = (
    ((2, 0, 4), 3),
    ((3, 0, 5), 11),
    ((5, 6, 7), 1),
    ((5, 4, 8), 21),
    ((6, 5, 9), 11),
    ((6, 26, 14, 10), 2),
    ((7, 4, 10), 3),
    ((7, 27, 15, 11), 7),
    ((8, 28, 16, 12), 2),
    ((9, 28, 16, 12), 5),
    ((9, 29, 17, 13), 4),
    ((10, 30, 17, 13), 3),
    ((10, 30, 18, 14), 6),
    ((11, 31, 19, 14), 2),
    ((11, 31, 19, 15), 9),
    ((12, 0, 20, 16), 7),
    ((13, 1, 21, 17), 9),
    ((14, 1, 21, 17), 4),
    ((14, 2, 22, 18), 2),
    ((15, 2, 22, 18), 7),
    ((17, 16, 20), 2),
    ((17, 4, 24, 20), 2),
    ((18, 6, 26, 22), 5),
    ((19, 16, 22), 4),
    ((19, 4, 24, 22), 1),
    ((20, 22, 23), 1),
    ((20, 27, 23), 2),
    ((21, 22, 23), 7),
    ((21, 20, 24), 12),
    ((22, 20, 24), 5),
    ((22, 21, 25), 1),
    ((23, 21, 25), 1),
    ((23, 24, 25), 5),
    ((23, 29, 25), 2),
    ((24, 27, 26), 7),
    ((25, 31, 27), 5),
    ((27, 24, 28), 9),
    ((28, 1, 29), 1),
)

RECEIVED = 20
OWN, MADE, TAKEN = 0, 16, 32
PASSED = TAKEN + RECEIVED


def row_range():
    top = 68.0 * math.pi / 180.0
    edge = math.log(math.tan(math.pi / 4 + top / 2))
    rows = np.arange(TOTAL)
    lat = 2.0 * np.arctan(np.exp(edge * (1.0 - (2 * rows + 1) / (2.0 * TOTAL)))) - math.pi / 2
    place = (top - lat) / top * TOTAL - 0.5
    first = np.clip(np.floor(place - 0.05), 0, TOTAL - 2).astype(int)
    last = np.clip(np.floor(place + 0.05), 0, TOTAL - 2).astype(int)
    return np.clip(first - 2, 0, TOTAL - 2), np.clip(last + 2, 0, TOTAL - 2) + 1


@functools.cache
def make_plan():
    low, high = row_range()
    flows = []
    head = [dict(sends=[], relays=[], locals=[], peers=set()) for _ in range(DEVICES)]
    made_first = {}
    for d in range(FIRST_BLENDED, DEVICES):
        for q in range(16 * d, 16 * d + 16):
            for s in range(low[8 * q] // LINES, min(high[8 * q + 7] // LINES, d - 1) + 1):
                made_first[s] = min(made_first.get(s, q), q)
    for r, h in enumerate(head):
        h["made_first"] = made_first.get(r, 0)
        h["made"] = 0
        h["extra"] = []
        h["used"] = [False] * RECEIVED
    for d in range(DEVICES):
        h = head[d]
        if d < FIRST_BLENDED:
            first, last = low[LINES * d] // 8, high[LINES * d + LINES - 1] // 8
            h["base"] = 8 * first
            h["count"] = last - first + 1
            for g in range(first, last + 1):
                flows.append((g // 16, d, OWN + g % 16, TAKEN + g - first))
        else:
            h["base"] = LINES * d
            for q in range(16 * d, 16 * d + 16):
                for n, s in enumerate(range(low[8 * q] // LINES, high[8 * q + 7] // LINES + 1)):
                    if s == d:
                        continue
                    place = q - made_first[s]
                    head[s]["made"] = max(head[s]["made"], place + 1)
                    if n == 0:
                        slot = q - 16 * d
                    else:
                        slot = 16 + len(h["extra"])
                        h["extra"].append(q - 16 * d)
                    flows.append((s, d, MADE + place, TAKEN + slot))
            h["count"] = 16 + len(h["extra"])
    routes = {}
    for way, blocks in ROUTES:
        routes.setdefault((way[0], way[-1]), []).extend([way] * blocks)
    passed = [0] * DEVICES
    for s, d, slot, goal in flows:
        head[d]["used"][goal - TAKEN] = True
        if s == d:
            head[s]["locals"].append((slot, goal))
            continue
        waiting = routes.get((s // 2, d // 2), [])
        way = waiting.pop() if waiting else (s // 2, d // 2)
        stops = []
        for chip in way[1:-1]:
            stop = min((2 * chip + s % 2, 2 * chip + 1 - s % 2), key=lambda v: passed[v])
            stops.append((stop, PASSED + passed[stop]))
            passed[stop] += 1
        stops.append((d, goal))
        at = s
        for leg, (stop, place) in enumerate(stops):
            if leg == 0:
                head[s]["sends"].append((-len(stops), slot, stop, place))
            else:
                head[at]["relays"].append((leg, -len(stops), slot, stop, place))
            head[at]["peers"].add(stop)
            head[stop]["peers"].add(at)
            at, slot = stop, place
    assert not any(routes.values())
    for h in head:
        inner = [i for i in range(16) if h["used"][i]]
        outer = [i for i in range(16, RECEIVED) if h["used"][i]]
        h["spans"] = []
        for some in (inner, outer):
            h["spans"] += [some[0], some[-1] + 1] if some else [0, 0]
            assert not some or len(some) == some[-1] + 1 - some[0]
        h["sends"] = [v[1:] for v in sorted(h["sends"], key=lambda v: v[0])]
        relays = sorted(h["relays"])
        h["early"] = sum(v[0] == 1 for v in relays)
        h["relays"] = [v[2:] for v in relays]
        h["peers"] = sorted(h["peers"])
    return head, max(passed)


(SENDS, EARLY, RELAYS, LOCALS, COUNT, MADE_COUNT, MADE_FIRST, BASE, EXTRAS, PEERS) = range(10)
SPANS, LISTS = 10, 14


def make_tables():
    head, most_passed = make_plan()
    width = lambda name: max(len(h[name]) for h in head)
    starts, at = {}, LISTS
    for name in ("extra", "peers", "locals", "sends", "relays"):
        starts[name] = at
        at += width(name) * (3 if name in ("locals", "sends", "relays") else 1)
    words = []
    for h in head:
        w = [None] * at
        w[SENDS], w[EARLY], w[RELAYS] = len(h["sends"]), h["early"], len(h["relays"])
        w[LOCALS], w[COUNT] = len(h["locals"]), int(h["count"])
        w[MADE_COUNT], w[MADE_FIRST] = int(h["made"]), int(h["made_first"])
        w[BASE], w[EXTRAS], w[PEERS] = int(h["base"]), len(h["extra"]), len(h["peers"])
        w[SPANS : SPANS + 4] = [int(v) for v in h["spans"]]
        for name in ("extra", "peers"):
            for i, v in enumerate(h[name]):
                w[starts[name] + i] = int(v)
        for i, (slot, place) in enumerate(h["locals"]):
            w[starts["locals"] + 3 * i : starts["locals"] + 3 * i + 3] = [int(slot), 0, int(place)]
        for name in ("sends", "relays"):
            for i, v in enumerate(h[name]):
                w[starts[name] + 3 * i : starts[name] + 3 * i + 3] = [int(x) for x in v]
        words.append(w)
    return words, starts, at, most_passed, width("sends"), width("relays")


def split(x):
    high = x.astype(jnp.bfloat16)
    return high, (x - high.astype(jnp.float32)).astype(jnp.bfloat16)


def mm(a, b):
    return jnp.dot(a, b, preferred_element_type=jnp.float32)


def weighted(weights, x):
    high, low = split(x)
    both = mm(weights, high)
    return both[:LINES] + both[LINES:] + mm(weights[:LINES], low)


def turned(row):
    return jnp.transpose(jnp.broadcast_to(row, (LINES, LINES)))


def kernel(
    words, starts, n_sends, most_extra,
    src, low_ref, weight_ref,
    merc, out1, out2, out3, out4,
    buf, tab, w_made, w_take, pool, tiles0, tiles1, tiles2, l3_send, l3_take,
    load_sem, send_sem, take_sem, y_send_sem, y_take_sem,
):
    r = lax.axis_index("rows")
    c = lax.axis_index("cols")

    def fill(low_half, count):
        if count == 1:
            for i, v in enumerate(words[low_half]):
                if v is not None:
                    tab[i] = v
            return
        half = count // 2
        lax.cond(
            r < low_half + half,
            lambda: fill(low_half, half),
            lambda: fill(low_half + half, half),
        )

    fill(0, DEVICES)

    def chunk(q):
        return pl.ds(q * CHUNK, CHUNK)

    loads = [
        pltpu.make_async_copy(
            src.at[:, :, chunk(q)], buf.at[q, pl.ds(OWN, 16)], load_sem.at[q]
        )
        for q in range(CHUNKS)
    ]
    for load in loads:
        load.start()

    barrier = pltpu.get_barrier_semaphore()
    n_peers = tab[PEERS]

    @pl.loop(0, n_peers)
    def _(i):
        pl.semaphore_signal(
            barrier, 1, device_id=(tab[starts["peers"] + i], c),
            device_id_type=pl.DeviceIdType.MESH,
        )

    for k in range(1, 4):
        pl.semaphore_signal(
            barrier, 1, device_id=(r, lax.rem(c + k, 4)), device_id_type=pl.DeviceIdType.MESH
        )

    n_made = tab[MADE_COUNT]

    @pl.when(n_made > 0)
    def _():
        first = tab[MADE_FIRST] * 8
        line, shift = first // LINES, lax.rem(first, LINES)
        after = jnp.minimum(line + 1, DEVICES - 1)
        lane = lax.broadcasted_iota(jnp.int32, (1, LINES), 1)

        def aligned(ref):
            one = pltpu.roll(jnp.broadcast_to(ref[pl.ds(line, 1), :], (8, LINES)), LINES - shift, 1)
            two = pltpu.roll(jnp.broadcast_to(ref[pl.ds(after, 1), :], (8, LINES)), LINES - shift, 1)
            return jnp.where(lane < LINES - shift, one[:1], two[:1])

        row = turned(aligned(low_ref))
        weight = turned(aligned(weight_ref))
        column = r * LINES + lax.broadcasted_iota(jnp.int32, (LINES, LINES), 1)
        values = jnp.where(row == column, weight, 0.0) + jnp.where(row + 1 == column, 1.0 - weight, 0.0)
        w_made[pl.ds(0, LINES), :], w_made[pl.ds(LINES, LINES), :] = split(values)

    pl.semaphore_wait(barrier, n_peers + 3)

    def copy(j, at, q):
        slot, device, place = tab[at], tab[at + 1], tab[at + 2]
        return pltpu.make_async_remote_copy(
            src_ref=buf.at[q, slot],
            dst_ref=buf.at[q, place],
            send_sem=send_sem.at[j, q],
            recv_sem=take_sem.at[place - TAKEN, q],
            device_id=(device, c),
            device_id_type=pl.DeviceIdType.MESH,
        )

    def arrived(place, q):
        return pltpu.make_async_remote_copy(
            src_ref=buf.at[q, place],
            dst_ref=buf.at[q, place],
            send_sem=send_sem.at[0, q],
            recv_sem=take_sem.at[place - TAKEN, q],
            device_id=(r, lax.rem(c + 1, 4)),
            device_id_type=pl.DeviceIdType.MESH,
        )

    n_own, n_locals = tab[SENDS], tab[LOCALS]
    for q in range(CHUNKS):
        loads[q].wait()

        @pl.when(n_made > 0)
        def _():
            @pl.loop(0, CHUNK // STEP)
            def _(t):
                columns = pl.ds(pl.multiple_of(t * STEP, STEP), STEP)
                x = buf[q, pl.ds(OWN, 16), :, columns].reshape(LINES, STEP)
                made = weighted(w_made[...], x)
                buf[q, pl.ds(MADE, 16), :, columns] = made.reshape(16, 8, STEP)

        @pl.loop(0, n_own)
        def _(j):
            copy(j, starts["sends"] + 3 * j, q).start()

        @pl.loop(0, n_locals)
        def _(i):
            place = tab[starts["locals"] + 3 * i + 2]
            pltpu.make_async_copy(
                src.at[tab[starts["locals"] + 3 * i], :, chunk(q)],
                buf.at[q, place],
                take_sem.at[place - TAKEN, q],
            ).start()

    blended = r >= FIRST_BLENDED
    n_taken = tab[COUNT]
    a = lax.broadcasted_iota(jnp.int32, (256, 128), 0)
    b = lax.broadcasted_iota(jnp.int32, (256, 128), 1)
    pool[...] = jnp.where(a // 2 == b, 0.25, 0.0).astype(jnp.bfloat16)

    @pl.when(jnp.logical_or(r < FIRST_BLENDED, r >= FIRST_KEPT))
    def _():
        row = turned(low_ref[pl.ds(r, 1), :]) - tab[BASE]
        weight = turned(weight_ref[pl.ds(r, 1), :])
        row = jnp.concatenate([row, row], axis=1)
        weight = jnp.concatenate([weight, weight], axis=1)
        column = lax.broadcasted_iota(jnp.int32, (LINES, 2 * LINES), 1)
        values = jnp.where(row == column, weight, 0.0) + jnp.where(row + 1 == column, 1.0 - weight, 0.0)
        high, low = split(values[:, : 8 * RECEIVED])
        w_take[pl.ds(0, LINES), :] = high
        w_take[pl.ds(LINES, LINES), :] = low

    n_early, n_relays = tab[EARLY], tab[RELAYS]

    def forward(j, q):
        at = starts["relays"] + 3 * j
        arrived(tab[at], q).wait_recv()
        copy(n_sends + j, at, q).start()

    for q in range(CHUNKS + 1):
        if q < CHUNKS:
            @pl.loop(0, n_early)
            def _(j):
                forward(j, q)
        if q > 0:
            @pl.loop(n_early, n_relays)
            def _(j):
                forward(j, q - 1)

    def pool_columns(blocks):
        rows = blocks[0].shape[0]
        high, low = split(jnp.concatenate(blocks, axis=0))
        both = mm(high, pool[...]) + mm(low, pool[...])
        return [both[rows * i : rows * i + rows] for i in range(len(blocks))]

    def halve(tiles, count, rows):
        def one(i):
            return tiles[i, pl.ds(0, rows, 2), :] + tiles[i, pl.ds(1, rows, 2), :]

        return pool_columns(
            [jnp.concatenate([one(i), one(i + 1)], axis=1) for i in range(0, count, 2)]
        )

    for q in range(CHUNKS):
        for span in (SPANS, SPANS + 2):
            @pl.loop(tab[span], tab[span + 1])
            def _(i):
                arrived(TAKEN + i, q).wait_recv()

        @pl.when(jnp.logical_not(blended))
        def _():
            for t in range(0, CHUNK, STEP):
                x = buf[q, pl.ds(TAKEN, RECEIVED), :, pl.ds(t, STEP)].reshape(8 * RECEIVED, STEP)
                x = jnp.where(lax.broadcasted_iota(jnp.int32, x.shape, 0) < 8 * n_taken, x, 0.0)
                merc[:, pl.ds(q * CHUNK + t, STEP)] = weighted(w_take[...], x)

        @pl.when(blended)
        def _():
            @pl.when(r < FIRST_KEPT)
            def _():
                merc[:, chunk(q)] = buf[q, pl.ds(TAKEN, 16)].reshape(LINES, CHUNK)

            @pl.when(r >= FIRST_KEPT)
            def _():
                for t in range(0, CHUNK, STEP):
                    x = buf[q, pl.ds(TAKEN, 16), :, pl.ds(t, STEP)].reshape(LINES, STEP)
                    x = jnp.where(lax.broadcasted_iota(jnp.int32, x.shape, 0) < 8 * tab[SPANS + 1], x, 0.0)
                    own = buf[q, pl.ds(OWN, 16), :, pl.ds(t, STEP)].reshape(LINES, STEP)
                    merc[:, pl.ds(q * CHUNK + t, STEP)] = x + weighted(w_take[:, :LINES], own)

            for i in range(most_extra):
                @pl.when(i < tab[EXTRAS])
                def _():
                    rows = pl.ds(pl.multiple_of(tab[starts["extra"] + i] * 8, 8), 8)
                    merc[rows, chunk(q)] += buf[q, TAKEN + 16 + i]

        for i in range(CHUNK // 128):
            tiles0[i] = merc[:, pl.ds(q * CHUNK + 128 * i, 128)]
        for i, part in enumerate(halve(tiles0, CHUNK // 128, 64)):
            tiles1[i] = part
            out1[:, pl.ds(q * CHUNK // 2 + 128 * i, 128)] = part
        for i, part in enumerate(halve(tiles1, CHUNK // 256, 32)):
            tiles2[i] = part
            out2[:, pl.ds(q * CHUNK // 4 + 128 * i, 128)] = part
        for i, part in enumerate(halve(tiles2, CHUNK // 512, 16)):
            for k in range(4):
                l3_send[k, :, pl.ds(q * CHUNK // 8 + 128 * i, 128)] = part[4 * k : 4 * k + 4]

    ys = []
    for k in range(1, 4):
        other = lax.rem(c + k, 4)
        ys.append(
            pltpu.make_async_remote_copy(
                src_ref=l3_send.at[other],
                dst_ref=l3_take.at[c],
                send_sem=y_send_sem.at[k - 1],
                recv_sem=y_take_sem.at[k - 1],
                device_id=(r, other),
                device_id_type=pl.DeviceIdType.MESH,
            )
        )
    for y in ys:
        y.start()
    for y in ys:
        y.wait_recv()
    for k in range(4):
        out3[:, pl.ds(k * WIDTH // 8, WIDTH // 8)] = jnp.where(c == k, l3_send[k], l3_take[k])
    level3 = out3[...]
    sums = jnp.concatenate(
        [level3[0:1] + level3[1:2], level3[2:3] + level3[3:4], jnp.zeros((6, WIDTH // 2), jnp.float32)],
        axis=0,
    )
    for i, part in enumerate(pool_columns([sums[:, 256 * i : 256 * i + 256] for i in range(16)])):
        out4[:, pl.ds(128 * i, 128)] = part[:2]

    for y in ys:
        y.wait_send()
    for q in range(CHUNKS):
        @pl.loop(0, n_own)
        def _(j):
            copy(j, starts["sends"] + 3 * j, q).wait_send()

        @pl.loop(0, n_relays)
        def _(j):
            copy(n_sends + j, starts["relays"] + 3 * j, q).wait_send()


def body(source, low_row, weight_low):
    words, starts, size, most_passed, n_sends, n_relays = make_tables()
    slots = PASSED + most_passed
    f32 = jnp.float32
    vmem = pl.BlockSpec(memory_space=pltpu.VMEM)
    return pl.pallas_call(
        functools.partial(kernel, words, starts, n_sends, starts["peers"] - starts["extra"]),
        out_shape=(
            jax.ShapeDtypeStruct((128, 8192), f32),
            jax.ShapeDtypeStruct((64, 4096), f32),
            jax.ShapeDtypeStruct((32, 2048), f32),
            jax.ShapeDtypeStruct((4, 4096), f32),
            jax.ShapeDtypeStruct((2, 2048), f32),
        ),
        in_specs=[pl.BlockSpec(memory_space=pl.ANY), vmem, vmem],
        out_specs=(vmem,) * 5,
        scratch_shapes=[
            pltpu.VMEM((CHUNKS, slots, 8, CHUNK), f32),
            pltpu.SMEM((size,), jnp.int32),
            pltpu.VMEM((2 * LINES, LINES), jnp.bfloat16),
            pltpu.VMEM((2 * LINES, 8 * RECEIVED), jnp.bfloat16),
            pltpu.VMEM((256, 128), jnp.bfloat16),
            pltpu.VMEM((CHUNK // 128, 128, 128), f32),
            pltpu.VMEM((CHUNK // 256, 64, 128), f32),
            pltpu.VMEM((CHUNK // 512, 32, 128), f32),
            pltpu.VMEM((4, 4, WIDTH // 8), f32),
            pltpu.VMEM((4, 4, WIDTH // 8), f32),
            pltpu.SemaphoreType.DMA((CHUNKS,)),
            pltpu.SemaphoreType.DMA((n_sends + n_relays, CHUNKS)),
            pltpu.SemaphoreType.DMA((RECEIVED + most_passed, CHUNKS)),
            pltpu.SemaphoreType.DMA((3,)),
            pltpu.SemaphoreType.DMA((3,)),
        ],
        compiler_params=pltpu.CompilerParams(
            collective_id=0, has_side_effects=True, vmem_limit_bytes=48 * 2**20
        ),
    )(source.reshape(16, 8, WIDTH), low_row.reshape(64, 128), weight_low.reshape(64, 128))


def solution(mesh):
    placed = (P("rows", "cols"), P(), P())
    return jax.shard_map(
        body,
        mesh=mesh,
        in_specs=placed,
        out_specs=(
            P("rows", "cols"),
            P("rows", "cols"),
            P("rows", "cols"),
            P(("rows", "cols"), None),
            P(("rows", "cols"), None),
        ),
        check_vma=False,
    )
```

time: 339 us -> 120 us (0.35); the launches traced: 333 us -> 120 us
  waiting for transfers between devices: 185 us -> 0 us
  Pallas kernels: 0 us -> 113 us
  local copies, waits for them, and re-layouts: 91.4 us -> 6.43 us
  other arithmetic: 27.1 us -> 0 us
  starting transfers between devices: 24.5 us -> 0 us
  matrix products: 3.4 us -> 0 us
    all_to_all x3 -> x0, waiting for transfers between devices: 185 us -> none  [the longest x1 92.7 us: body(): lax.all_to_all(blended, 'rows', split_axis=0, concat_axis=1, tiled=True)]
    pallas_call x0 -> x1, Pallas kernels: none -> 113 us  [body(): pl.pallas_call(functools.partial(kernel, words, starts, n_sends, starts['...]
    gather x1 -> x0, local copies, waits for them, and re-layouts: 56.6 us -> none  [blend(): fetched = jnp.take(columns, both_rows, axis=0)]
    all_to_all x3 -> x0, starting transfers between devices: 24.5 us -> none  [the longest x1 11 us: body(): lax.all_to_all(source, 'rows', split_axis=1, concat_axis=0, tiled=True)]
    all_to_all x5 -> x0, local copies, waits for them, and re-layouts: 17.7 us -> none  [the longest x2 12.2 us: body(): lax.all_to_all(blended, 'rows', split_axis=0, concat_axis=1, tiled=True)]
    add x6 -> x0, other arithmetic: 15.2 us -> none  [the longest x4 11.4 us: halve(): row_sums = stacked[:, 0, :] + stacked[:, 1, :]]
    select_n x2 -> x0, other arithmetic: 11.8 us -> none  [blend(): fetched = jnp.take(columns, both_rows, axis=0)]
    reshape x2 -> x0, local copies, waits for them, and re-layouts: 5.86 us -> none  [halve(): stacked = picture.reshape(height // 2, 2, width)]
  transfers between devices with their start and end apart: 3 -> 0, of which waited for: 2 -> 0; matrix products, arithmetic and copies ran while one was open for 4% -> 0% of each run, Pallas kernels for 0% -> 0%
where the time goes in v1:
time: 120 us
  Pallas kernels  113 us (94%)
  local copies, waits for them, and re-layouts  6.43 us (5%)
    pallas_call x1, Pallas kernels, body(): pl.pallas_call(functools.partial(kernel, words, starts, n_sends, starts['...  113 us
    unnamed x9, local copies, waits for them, and re-layouts  6.43 us

profile of v1, /device:TPU:102, one launch (start us, length us, event | category | flops | bytes accessed | tf_op | source)
XLA Modules:
  0.0 120.3 jit_solution(10413684916361302696)
XLA Ops:
  0.6 0.0 copy-start
  0.6 0.7 copy-done
  1.4 0.0 copy-start.1
  1.4 0.8 copy-done.1
  2.1 113.2 %shard_map.74 = (f32[128,8192]{1,0:T(8,128)S(1)}, f32[64,4096]{1,0:T(8,128)S(1)}, f32[32,2048]{1,0:T(8,128)S(1)}, f32[4,4096]{1,0:T(4,128)S(1)}, f32[2,2048]{1,0:T(2,128)S(1)}) custom-call(f32[16,8,8192]{2,1,0:T(8,128)} %bitcast.5, s32[64,128]{1,0:T(8,128)S(1)} %bitcast.3, f32[64,128]{1,0:T(8,128)S(1)} %bitcast.4), custom_call_target="tpu_custom_call" | custom-call | tf_op jit(solution)/shard_map/pallas_call | solution.py:468
  115.4 2.0 %copy.13 = f32[128,8192]{1,0:T(8,128)} copy(f32[128,8192]{1,0:T(8,128)S(1)} %get-tuple-element.10) | data formatting | bytes 8388608
  117.4 1.0 copy.14
  118.3 0.7 copy.15
  119.0 0.6 copy.16
  119.7 0.6 copy.17
Async XLA Ops:
  0.6 0.8 copy-start
  1.4 0.8 copy-start.1

commit v2 on v1

--- a/solution.py
+++ b/solution.py
@@ -20,44 +20,39 @@
 STEP = 1024
 
 ROUTES = (
-    ((2, 0, 4), 3),
+    ((2, 0, 4), 2),
     ((3, 0, 5), 11),
-    ((5, 6, 7), 1),
     ((5, 4, 8), 21),
-    ((6, 5, 9), 11),
-    ((6, 26, 14, 10), 2),
-    ((7, 4, 10), 3),
-    ((7, 27, 15, 11), 7),
-    ((8, 28, 16, 12), 2),
+    ((6, 5, 9), 12),
+    ((7, 4, 10), 4),
+    ((7, 27, 15, 11), 5),
+    ((8, 28, 16, 12), 1),
     ((9, 28, 16, 12), 5),
-    ((9, 29, 17, 13), 4),
+    ((9, 29, 17, 13), 3),
     ((10, 30, 17, 13), 3),
-    ((10, 30, 18, 14), 6),
+    ((10, 30, 18, 14), 5),
     ((11, 31, 19, 14), 2),
-    ((11, 31, 19, 15), 9),
-    ((12, 0, 20, 16), 7),
-    ((13, 1, 21, 17), 9),
-    ((14, 1, 21, 17), 4),
-    ((14, 2, 22, 18), 2),
-    ((15, 2, 22, 18), 7),
-    ((17, 16, 20), 2),
-    ((17, 4, 24, 20), 2),
-    ((18, 6, 26, 22), 5),
-    ((19, 16, 22), 4),
-    ((19, 4, 24, 22), 1),
-    ((20, 22, 23), 1),
+    ((11, 31, 19, 15), 8),
+    ((12, 0, 20, 16), 6),
+    ((13, 1, 21, 17), 8),
+    ((14, 2, 22, 17), 5),
+    ((15, 2, 22, 18), 6),
+    ((17, 16, 20), 5),
+    ((18, 17, 21), 2),
+    ((18, 6, 26, 22), 2),
+    ((19, 16, 22), 2),
+    ((19, 6, 26, 22), 1),
+    ((19, 7, 27, 23), 1),
     ((20, 27, 23), 2),
     ((21, 22, 23), 7),
-    ((21, 20, 24), 12),
-    ((22, 20, 24), 5),
-    ((22, 21, 25), 1),
-    ((23, 21, 25), 1),
+    ((21, 20, 24), 14),
+    ((22, 20, 24), 4),
+    ((22, 21, 25), 3),
     ((23, 24, 25), 5),
-    ((23, 29, 25), 2),
-    ((24, 27, 26), 7),
-    ((25, 31, 27), 5),
-    ((27, 24, 28), 9),
-    ((28, 1, 29), 1),
+    ((24, 22, 26), 1),
+    ((24, 27, 26), 5),
+    ((25, 31, 27), 2),
+    ((27, 24, 28), 8),
 )
 
 RECEIVED = 20
@@ -114,17 +109,27 @@
                         h["extra"].append(q - 16 * d)
                     flows.append((s, d, MADE + place, TAKEN + slot))
             h["count"] = 16 + len(h["extra"])
+    between = {}
+    for s, d, _, _ in flows:
+        between[s // 2, d // 2] = between.get((s // 2, d // 2), 0) + 1
+    ways = {}
+    for way, blocks in ROUTES:
+        ways.setdefault((way[0], way[-1]), []).append([blocks, way])
     routes = {}
-    for way, blocks in ROUTES:
-        routes.setdefault((way[0], way[-1]), []).extend([way] * blocks)
+    for pair, total in between.items():
+        counts = ways.get(pair, [])
+        rest = total - sum(n for n, _ in counts)
+        assert rest >= 0
+        marks = [((i + 0.5) / n, way) for n, way in counts + [[rest, pair]] for i in range(n)]
+        routes[pair] = [way for _, way in sorted(marks)]
     passed = [0] * DEVICES
     for s, d, slot, goal in flows:
         head[d]["used"][goal - TAKEN] = True
         if s == d:
             head[s]["locals"].append((slot, goal))
+            routes[s // 2, d // 2].pop()
             continue
-        waiting = routes.get((s // 2, d // 2), [])
-        way = waiting.pop() if waiting else (s // 2, d // 2)
+        way = routes[s // 2, d // 2].pop()
         stops = []
         for chip in way[1:-1]:
             stop = min((2 * chip + s % 2, 2 * chip + 1 - s % 2), key=lambda v: passed[v])
@@ -148,7 +153,14 @@
         for some in (inner, outer):
             h["spans"] += [some[0], some[-1] + 1] if some else [0, 0]
             assert not some or len(some) == some[-1] + 1 - some[0]
-        h["sends"] = [v[1:] for v in sorted(h["sends"], key=lambda v: v[0])]
+        turns, seen = [], {}
+        for stops, *move in sorted(h["sends"], key=lambda v: v[0]):
+            key = stops, move[1]
+            seen[key] = seen.get(key, 0) + 1
+            turns.append((stops == -1, key, seen[key], move))
+        h["sends"] = [
+            move for _, _, _, move in sorted(turns, key=lambda v: (v[0], (v[2] - 0.5) / seen[v[1]], v[1]))
+        ]
         relays = sorted(h["relays"])
         h["early"] = sum(v[0] == 1 for v in relays)
         h["relays"] = [v[2:] for v in relays]
@@ -460,12 +472,26 @@
             copy(n_sends + j, starts["relays"] + 3 * j, q).wait_send()
 
 
+def store(*refs):
+    *arrays, sems = refs
+    copies = []
+    for i in range(4):
+        rows = pl.ds(32 * i, 32)
+        copies.append(pltpu.make_async_copy(arrays[0].at[rows], arrays[5].at[rows], sems.at[i]))
+    for i in range(1, 5):
+        copies.append(pltpu.make_async_copy(arrays[i], arrays[5 + i], sems.at[3 + i]))
+    for copy in copies:
+        copy.start()
+    for copy in copies:
+        copy.wait()
+
+
 def body(source, low_row, weight_low):
     words, starts, size, most_passed, n_sends, n_relays = make_tables()
     slots = PASSED + most_passed
     f32 = jnp.float32
     vmem = pl.BlockSpec(memory_space=pltpu.VMEM)
-    return pl.pallas_call(
+    results = pl.pallas_call(
         functools.partial(kernel, words, starts, n_sends, starts["peers"] - starts["extra"]),
         out_shape=(
             jax.ShapeDtypeStruct((128, 8192), f32),
@@ -497,6 +523,14 @@
             collective_id=0, has_side_effects=True, vmem_limit_bytes=48 * 2**20
         ),
     )(source.reshape(16, 8, WIDTH), low_row.reshape(64, 128), weight_low.reshape(64, 128))
+    return pl.pallas_call(
+        store,
+        out_shape=tuple(jax.ShapeDtypeStruct(v.shape, v.dtype) for v in results),
+        in_specs=[vmem] * 5,
+        out_specs=(pl.BlockSpec(memory_space=pl.ANY),) * 5,
+        scratch_shapes=[pltpu.SemaphoreType.DMA((8,))],
+        compiler_params=pltpu.CompilerParams(vmem_limit_bytes=2**20),
+    )(*results)
 
 
 def solution(mesh):

time: 120 us -> 106 us (0.88)
  Pallas kernels: 113 us -> 104 us
  local copies, waits for them, and re-layouts: 6.43 us -> 1.51 us
    pallas_call x1, Pallas kernels: 113 us -> 101 us  [body(): pl.pallas_call(functools.partial(kernel, words, starts, n_sends, starts['...]
    unnamed x9 -> x4, local copies, waits for them, and re-layouts: 6.43 us -> 1.51 us
    pallas_call x0 -> x1, Pallas kernels: none -> 2.48 us  [body(): pl.pallas_call(store, out_shape=tuple((jax.ShapeDtypeStruct(v.shape, v.dt...]
where the time goes in v2:
time: 106 us
  Pallas kernels  104 us (98%)
  local copies, waits for them, and re-layouts  1.51 us (1%)
    pallas_call x1, Pallas kernels, body(): pl.pallas_call(functools.partial(kernel, words, starts, n_sends, starts['...  101 us
    pallas_call x1, Pallas kernels, body(): pl.pallas_call(store, out_shape=tuple((jax.ShapeDtypeStruct(v.shape, v.dt...  2.48 us

profile of v2, /device:TPU:102, one launch (start us, length us, event | category | flops | bytes accessed | tf_op | source)
XLA Modules:
  0.0 105.8 jit_solution(12600311274025481267)
XLA Ops:
  0.6 0.0 copy-start
  0.6 0.7 copy-done
  1.4 0.0 copy-start.1
  1.4 0.8 copy-done.1
  2.1 101.1 %shard_map.74 = (f32[128,8192]{1,0:T(8,128)S(1)}, f32[64,4096]{1,0:T(8,128)S(1)}, f32[32,2048]{1,0:T(8,128)S(1)}, f32[4,4096]{1,0:T(4,128)S(1)}, f32[2,2048]{1,0:T(2,128)S(1)}) custom-call(f32[16,8,8192]{2,1,0:T(8,128)} %bitcast.5, s32[64,128]{1,0:T(8,128)S(1)} %bitcast.3, f32[64,128]{1,0:T(8,128)S(1)} %bitcast.4), custom_call_target="tpu_custom_call" | custom-call | tf_op jit(solution)/shard_map/pallas_call | solution.py:494
  103.3 2.5 %shard_map.75 = (f32[128,8192]{1,0:T(8,128)}, f32[64,4096]{1,0:T(8,128)}, f32[32,2048]{1,0:T(8,128)}, f32[4,4096]{1,0:T(4,128)}, f32[2,2048]{1,0:T(2,128)}) custom-call(f32[128,8192]{1,0:T(8,128)S(1)} %get-tuple-element.10.refs_0_, f32[64,4096]{1,0:T(8,128)S(1)} %get-tuple-element.11.refs_1_, f32[32,2048]{1,0:T(8,128)S(1)} %get-tuple-element.12.refs_2_, ...), custom_call_target="tpu_custom_call" | custom-call | tf_op jit(solution)/shard_map/pallas_call | solution.py:526
Async XLA Ops:
  0.6 0.8 copy-start
  1.4 0.8 copy-start.1

commit v3 on v2

--- a/solution.py
+++ b/solution.py
@@ -20,39 +20,43 @@
 STEP = 1024
 
 ROUTES = (
-    ((2, 0, 4), 2),
-    ((3, 0, 5), 11),
-    ((5, 4, 8), 21),
-    ((6, 5, 9), 12),
-    ((7, 4, 10), 4),
-    ((7, 27, 15, 11), 5),
-    ((8, 28, 16, 12), 1),
-    ((9, 28, 16, 12), 5),
-    ((9, 29, 17, 13), 3),
-    ((10, 30, 17, 13), 3),
-    ((10, 30, 18, 14), 5),
-    ((11, 31, 19, 14), 2),
-    ((11, 31, 19, 15), 8),
-    ((12, 0, 20, 16), 6),
-    ((13, 1, 21, 17), 8),
-    ((14, 2, 22, 17), 5),
-    ((15, 2, 22, 18), 6),
-    ((17, 16, 20), 5),
-    ((18, 17, 21), 2),
-    ((18, 6, 26, 22), 2),
-    ((19, 16, 22), 2),
-    ((19, 6, 26, 22), 1),
-    ((19, 7, 27, 23), 1),
+    ((2, 5, 4), 1),
+    ((3, 1, 5), 12),
+    ((4, 3, 7), 1),
+    ((5, 6, 7), 1),
+    ((5, 4, 8), 17),
+    ((6, 5, 9), 10),
+    ((7, 4, 10), 1),
+    ((7, 23, 10), 6),
+    ((9, 8, 12), 1),
+    ((9, 28, 12), 4),
+    ((9, 29, 13), 1),
+    ((10, 30, 14), 6),
+    ((11, 31, 15), 8),
+    ((12, 28, 16), 4),
+    ((13, 28, 16), 3),
+    ((13, 29, 17), 3),
+    ((14, 30, 18), 3),
+    ((15, 31, 19), 4),
+    ((17, 16, 20), 2),
+    ((18, 16, 21), 2),
+    ((18, 17, 21), 1),
+    ((19, 16, 22), 3),
+    ((19, 18, 22), 1),
+    ((19, 20, 22), 2),
+    ((20, 19, 23), 2),
     ((20, 27, 23), 2),
     ((21, 22, 23), 7),
-    ((21, 20, 24), 14),
-    ((22, 20, 24), 4),
-    ((22, 21, 25), 3),
-    ((23, 24, 25), 5),
-    ((24, 22, 26), 1),
-    ((24, 27, 26), 5),
-    ((25, 31, 27), 2),
-    ((27, 24, 28), 8),
+    ((21, 16, 24), 2),
+    ((21, 20, 24), 9),
+    ((22, 20, 24), 2),
+    ((22, 23, 24), 4),
+    ((23, 20, 25), 5),
+    ((23, 29, 25), 5),
+    ((24, 27, 26), 8),
+    ((25, 31, 27), 7),
+    ((27, 24, 28), 10),
+    ((28, 31, 29), 2),
 )
 
 RECEIVED = 20
@@ -122,6 +126,11 @@
         assert rest >= 0
         marks = [((i + 0.5) / n, way) for n, way in counts + [[rest, pair]] for i in range(n)]
         routes[pair] = [way for _, way in sorted(marks)]
+    loads, sides = [0] * DEVICES, {}
+    for way, blocks in sorted(ROUTES, key=lambda v: -v[1]):
+        for chip in way[1:-1]:
+            sides[way, chip] = int(loads[2 * chip + 1] < loads[2 * chip])
+            loads[2 * chip + sides[way, chip]] += blocks
     passed = [0] * DEVICES
     for s, d, slot, goal in flows:
         head[d]["used"][goal - TAKEN] = True
@@ -132,7 +141,7 @@
         way = routes[s // 2, d // 2].pop()
         stops = []
         for chip in way[1:-1]:
-            stop = min((2 * chip + s % 2, 2 * chip + 1 - s % 2), key=lambda v: passed[v])
+            stop = 2 * chip + sides[way, chip]
             stops.append((stop, PASSED + passed[stop]))
             passed[stop] += 1
         stops.append((d, goal))

time: 106 us -> 100 us (0.943)
  Pallas kernels: 104 us -> 97.1 us
    pallas_call x1, Pallas kernels: 101 us -> 94.6 us  [body(): pl.pallas_call(functools.partial(kernel, words, starts, n_sends, starts['...]
where the time goes in v3:
time: 100 us; the launch traced here: 99.2 us
  Pallas kernels  97.1 us (97%)
  local copies, waits for them, and re-layouts  1.51 us (2%)
    pallas_call x1, Pallas kernels, body(): pl.pallas_call(functools.partial(kernel, words, starts, n_sends, starts['...  94.6 us
    pallas_call x1, Pallas kernels, body(): pl.pallas_call(store, out_shape=tuple((jax.ShapeDtypeStruct(v.shape, v.dt...  2.48 us

profile of v3, /device:TPU:102, one launch (start us, length us, event | category | flops | bytes accessed | tf_op | source)
XLA Modules:
  0.0 99.2 jit_solution(7715661324558947377)
XLA Ops:
  0.6 0.0 copy-start
  0.6 0.7 copy-done
  1.4 0.0 copy-start.1
  1.4 0.8 copy-done.1
  2.1 94.6 %shard_map.74 = (f32[128,8192]{1,0:T(8,128)S(1)}, f32[64,4096]{1,0:T(8,128)S(1)}, f32[32,2048]{1,0:T(8,128)S(1)}, f32[4,4096]{1,0:T(4,128)S(1)}, f32[2,2048]{1,0:T(2,128)S(1)}) custom-call(f32[16,8,8192]{2,1,0:T(8,128)} %bitcast.5, s32[64,128]{1,0:T(8,128)S(1)} %bitcast.3, f32[64,128]{1,0:T(8,128)S(1)} %bitcast.4), custom_call_target="tpu_custom_call" | custom-call | tf_op jit(solution)/shard_map/pallas_call | solution.py:503
  96.7 2.5 %shard_map.75 = (f32[128,8192]{1,0:T(8,128)}, f32[64,4096]{1,0:T(8,128)}, f32[32,2048]{1,0:T(8,128)}, f32[4,4096]{1,0:T(4,128)}, f32[2,2048]{1,0:T(2,128)}) custom-call(f32[128,8192]{1,0:T(8,128)S(1)} %get-tuple-element.10.refs_0_, f32[64,4096]{1,0:T(8,128)S(1)} %get-tuple-element.11.refs_1_, f32[32,2048]{1,0:T(8,128)S(1)} %get-tuple-element.12.refs_2_, ...), custom_call_target="tpu_custom_call" | custom-call | tf_op jit(solution)/shard_map/pallas_call | solution.py:535
Async XLA Ops:
  0.6 0.8 copy-start
  1.4 0.8 copy-start.1

commit v4 on v3

--- a/solution.py
+++ b/solution.py
@@ -20,43 +20,35 @@
 STEP = 1024
 
 ROUTES = (
-    ((2, 5, 4), 1),
-    ((3, 1, 5), 12),
-    ((4, 3, 7), 1),
-    ((5, 6, 7), 1),
-    ((5, 4, 8), 17),
-    ((6, 5, 9), 10),
-    ((7, 4, 10), 1),
-    ((7, 23, 10), 6),
-    ((9, 8, 12), 1),
-    ((9, 28, 12), 4),
-    ((9, 29, 13), 1),
-    ((10, 30, 14), 6),
-    ((11, 31, 15), 8),
-    ((12, 28, 16), 4),
-    ((13, 28, 16), 3),
-    ((13, 29, 17), 3),
-    ((14, 30, 18), 3),
-    ((15, 31, 19), 4),
-    ((17, 16, 20), 2),
-    ((18, 16, 21), 2),
-    ((18, 17, 21), 1),
-    ((19, 16, 22), 3),
-    ((19, 18, 22), 1),
-    ((19, 20, 22), 2),
-    ((20, 19, 23), 2),
-    ((20, 27, 23), 2),
+    ((2, 0, 4), 1),
+    ((3, 0, 5), 12),
+    ((4, 11, 7), 2),
+    ((5, 4, 8), 19),
+    ((6, 5, 9), 11),
+    ((7, 4, 11), 1),
+    ((7, 23, 11), 7),
+    ((9, 29, 13), 7),
+    ((10, 30, 14), 7),
+    ((11, 31, 15), 9),
+    ((12, 28, 16), 5),
+    ((13, 29, 17), 7),
+    ((14, 30, 17), 4),
+    ((15, 31, 18), 5),
+    ((17, 19, 20), 2),
+    ((18, 16, 21), 3),
+    ((19, 16, 22), 5),
+    ((20, 27, 23), 4),
     ((21, 22, 23), 7),
-    ((21, 16, 24), 2),
     ((21, 20, 24), 9),
-    ((22, 20, 24), 2),
-    ((22, 23, 24), 4),
-    ((23, 20, 25), 5),
-    ((23, 29, 25), 5),
-    ((24, 27, 26), 8),
-    ((25, 31, 27), 7),
-    ((27, 24, 28), 10),
-    ((28, 31, 29), 2),
+    ((21, 28, 24), 8),
+    ((22, 20, 24), 7),
+    ((22, 21, 25), 4),
+    ((23, 24, 25), 6),
+    ((24, 22, 26), 9),
+    ((25, 26, 27), 1),
+    ((26, 1, 28), 1),
+    ((27, 24, 28), 9),
+    ((28, 1, 29), 2),
 )
 
 RECEIVED = 20

time: 100 us -> 97.8 us (0.978)
  Pallas kernels: 97.1 us -> 94.3 us
    pallas_call x1, Pallas kernels: 94.6 us -> 91.8 us  [body(): pl.pallas_call(functools.partial(kernel, words, starts, n_sends, starts['...]
where the time goes in v4:
time: 97.8 us; the launch traced here: 96.5 us
  Pallas kernels  94.3 us (96%)
  local copies, waits for them, and re-layouts  1.51 us (2%)
    pallas_call x1, Pallas kernels, body(): pl.pallas_call(functools.partial(kernel, words, starts, n_sends, starts['...  91.8 us
    pallas_call x1, Pallas kernels, body(): pl.pallas_call(store, out_shape=tuple((jax.ShapeDtypeStruct(v.shape, v.dt...  2.48 us

profile of v4, /device:TPU:102, one launch (start us, length us, event | category | flops | bytes accessed | tf_op | source)
XLA Modules:
  0.0 96.5 jit_solution(4866207640531719000)
XLA Ops:
  0.6 0.0 copy-start
  0.6 0.7 copy-done
  1.4 0.0 copy-start.1
  1.4 0.8 copy-done.1
  2.1 91.8 %shard_map.74 = (f32[128,8192]{1,0:T(8,128)S(1)}, f32[64,4096]{1,0:T(8,128)S(1)}, f32[32,2048]{1,0:T(8,128)S(1)}, f32[4,4096]{1,0:T(4,128)S(1)}, f32[2,2048]{1,0:T(2,128)S(1)}) custom-call(f32[16,8,8192]{2,1,0:T(8,128)} %bitcast.5, s32[64,128]{1,0:T(8,128)S(1)} %bitcast.3, f32[64,128]{1,0:T(8,128)S(1)} %bitcast.4), custom_call_target="tpu_custom_call" | custom-call | tf_op jit(solution)/shard_map/pallas_call | solution.py:495
  94.0 2.5 %shard_map.75 = (f32[128,8192]{1,0:T(8,128)}, f32[64,4096]{1,0:T(8,128)}, f32[32,2048]{1,0:T(8,128)}, f32[4,4096]{1,0:T(4,128)}, f32[2,2048]{1,0:T(2,128)}) custom-call(f32[128,8192]{1,0:T(8,128)S(1)} %get-tuple-element.10.refs_0_, f32[64,4096]{1,0:T(8,128)S(1)} %get-tuple-element.11.refs_1_, f32[32,2048]{1,0:T(8,128)S(1)} %get-tuple-element.12.refs_2_, ...), custom_call_target="tpu_custom_call" | custom-call | tf_op jit(solution)/shard_map/pallas_call | solution.py:527
Async XLA Ops:
  0.6 0.8 copy-start
  1.4 0.8 copy-start.1

commit v5 on v4

--- a/solution.py
+++ b/solution.py
@@ -291,8 +291,6 @@
         values = jnp.where(row == column, weight, 0.0) + jnp.where(row + 1 == column, 1.0 - weight, 0.0)
         w_made[pl.ds(0, LINES), :], w_made[pl.ds(LINES, LINES), :] = split(values)
 
-    pl.semaphore_wait(barrier, n_peers + 3)
-
     def copy(j, at, q):
         slot, device, place = tab[at], tab[at + 1], tab[at + 2]
         return pltpu.make_async_remote_copy(
@@ -326,6 +324,9 @@
                 x = buf[q, pl.ds(OWN, 16), :, columns].reshape(LINES, STEP)
                 made = weighted(w_made[...], x)
                 buf[q, pl.ds(MADE, 16), :, columns] = made.reshape(16, 8, STEP)
+
+        if q == 0:
+            pl.semaphore_wait(barrier, n_peers + 3)
 
         @pl.loop(0, n_own)
         def _(j):

time: 97.8 us -> 97.8 us (level)
  no operation moved by 1% of the time
where the time goes in v5:
time: 97.8 us; the launch traced here: 96.5 us
  Pallas kernels  94.3 us (96%)
  local copies, waits for them, and re-layouts  1.51 us (2%)
    pallas_call x1, Pallas kernels, body(): pl.pallas_call(functools.partial(kernel, words, starts, n_sends, starts['...  91.8 us
    pallas_call x1, Pallas kernels, body(): pl.pallas_call(store, out_shape=tuple((jax.ShapeDtypeStruct(v.shape, v.dt...  2.48 us

profile of v5, /device:TPU:102, one launch (start us, length us, event | category | flops | bytes accessed | tf_op | source)
XLA Modules:
  0.0 96.5 jit_solution(12576964553892926945)
XLA Ops:
  0.6 0.0 copy-start
  0.6 0.7 copy-done
  1.4 0.0 copy-start.1
  1.4 0.8 copy-done.1
  2.1 91.8 %shard_map.74 = (f32[128,8192]{1,0:T(8,128)S(1)}, f32[64,4096]{1,0:T(8,128)S(1)}, f32[32,2048]{1,0:T(8,128)S(1)}, f32[4,4096]{1,0:T(4,128)S(1)}, f32[2,2048]{1,0:T(2,128)S(1)}) custom-call(f32[16,8,8192]{2,1,0:T(8,128)} %bitcast.5, s32[64,128]{1,0:T(8,128)S(1)} %bitcast.3, f32[64,128]{1,0:T(8,128)S(1)} %bitcast.4), custom_call_target="tpu_custom_call" | custom-call | tf_op jit(solution)/shard_map/pallas_call | solution.py:496
  94.0 2.5 %shard_map.75 = (f32[128,8192]{1,0:T(8,128)}, f32[64,4096]{1,0:T(8,128)}, f32[32,2048]{1,0:T(8,128)}, f32[4,4096]{1,0:T(4,128)}, f32[2,2048]{1,0:T(2,128)}) custom-call(f32[128,8192]{1,0:T(8,128)S(1)} %get-tuple-element.10.refs_0_, f32[64,4096]{1,0:T(8,128)S(1)} %get-tuple-element.11.refs_1_, f32[32,2048]{1,0:T(8,128)S(1)} %get-tuple-element.12.refs_2_, ...), custom_call_target="tpu_custom_call" | custom-call | tf_op jit(solution)/shard_map/pallas_call | solution.py:528
Async XLA Ops:
  0.6 0.8 copy-start
  1.4 0.8 copy-start.1
